TPU v7x, 32 devices: a whole 2x2x4 slice. The times are simulated.
32 devices in a mesh: trade: 4 (over z), node: 8 (over y, x, core).
Axes of the slice: x: 2, y: 2, z: 4, core: 2. Of those that a mesh axis runs over, the one named last changes fastest.
Arguments:
- values_in: float32 [1024, 16384], P('trade', 'node'), may hold values from 0 to 1
- prob_up: float32 [16, 16384], P(None, 'node'), may hold values from 0.1 to 0.3
- prob_down: float32 [16, 16384], P(None, 'node'), may hold values from 0.1 to 0.3
- discount: float32 [16, 16384], P(None, 'node'), may hold values from 0.9 to 1
- swap_rate: float32 [16, 16384], P(None, 'node'), may hold values from -3 to 3
- annuity: float32 [16, 16384], P(None, 'node'), may hold values from 0.5 to 2
- state_price: float32 [16384], P('node'), may hold values from 3.0517578e-05 to 0.00012207031
- exercise_step: int32 [1024, 4], P('trade'), may hold values from 0 to 15
- strike_bucket: int32 [1024], P('trade'), may hold values from 0 to 63
- notional_sign: int32 [1024], P('trade'), may hold values from 0 to 1
- strike_table: float32 [64], replicated, may hold values from -0.5 to 0.5
Outputs:
- values_out: float32 [1024, 16384], P(('trade', 'node'))
- prices: float32 [1024], P(('trade', 'node'))
- portfolio: float32 [], replicated
All inputs are finite; a program needn't handle non-finite values.
Results may differ from a plain program's by a relative error of at most 0.0003.
Values sent between devices are 32-bit elements; how exact they have to be, the bound alone decides.
A program may use at most 128 MiB of HBM per device.

v0:
```python
import jax
import jax.numpy as jnp
from jax import lax
from jax.sharding import PartitionSpec as P


def strikes_of(bucket, strike_table):
    levels = lax.broadcasted_iota(jnp.int32, (1, strike_table.shape[0]), 1)
    return jnp.sum(
        jnp.where(
            bucket[:, None] == levels, strike_table[None, :], jnp.zeros((), strike_table.dtype)
        ),
        axis=1,
    )


def roll_once(padded, prob_up, prob_down, discount_row):
    middle = 1.0 - prob_up - prob_down
    return discount_row * (
        prob_up * padded[:, 2:] + middle * padded[:, 1:-1] + prob_down * padded[:, :-2]
    )


def exercise(values, active, strike, signs, swap_row, annuity_row):
    payoff = signs[:, None] * annuity_row[None, :] * (swap_row[None, :] - strike[:, None])
    return jnp.where(active[:, None], jnp.maximum(values, payoff), values)


def stack_lattice(prob_up, prob_down, discount, swap_rate, annuity, state_price, first_step):
    span = prob_up.shape[0] - first_step
    spread_price = jnp.broadcast_to(state_price[None, :], (span, state_price.shape[0]))
    return jnp.stack([prob_up, prob_down, discount, swap_rate, annuity, spread_price])


def to_trade_rows(values):
    node_count = lax.axis_size("node")
    node_dev = values.shape[1]
    row_count = values.shape[0] // node_count
    blocks = values.reshape(node_count, row_count, node_dev)
    moved = lax.all_to_all(blocks, "node", split_axis=0, concat_axis=2, tiled=True)
    return moved.reshape(row_count, node_dev * node_count)


def roll_back(values, lattice, exercise_step, strike, signs, split_step, step_count):
    row_count = values.shape[0]
    first_row = lax.axis_index("node") * row_count
    my_dates = lax.dynamic_slice_in_dim(exercise_step, first_row, row_count, 0)
    my_strike = lax.dynamic_slice_in_dim(strike, first_row, row_count, 0)
    my_signs = lax.dynamic_slice_in_dim(signs, first_row, row_count, 0)
    for step in range(split_step, step_count):
        local_step = step - split_step
        padded = jnp.pad(values, ((0, 0), (1, 1)))
        values = roll_once(
            padded, lattice[0, local_step], lattice[1, local_step], lattice[2, local_step]
        )
        active = jnp.any(my_dates == step, axis=1)
        values = exercise(
            values, active, my_strike, my_signs, lattice[3, local_step], lattice[4, local_step]
        )
    prices = jnp.sum(values * lattice[5, 0][None, :], axis=1)
    return (values, prices)


def local(
    values_in,
    prob_up,
    prob_down,
    discount,
    swap_rate,
    annuity,
    state_price,
    exercise_step,
    strike_bucket,
    notional_sign,
    strike_table,
):
    step_count = prob_up.shape[0]
    strike = strikes_of(strike_bucket, strike_table)
    signs = (2 * notional_sign - 1).astype(jnp.float32)
    values = to_trade_rows(values_in)
    local_lattice = stack_lattice(prob_up, prob_down, discount, swap_rate, annuity, state_price, 0)
    lattice = lax.all_gather(local_lattice, "node", axis=2, tiled=True)
    values, prices = roll_back(values, lattice, exercise_step, strike, signs, 0, step_count)
    portfolio = lax.psum(jnp.sum(prices), ("trade", "node")) / values_in.shape[0]
    return (values, prices, portfolio)


def solution(mesh):
    in_specs = (
        P("trade", "node"),
        P(None, "node"),
        P(None, "node"),
        P(None, "node"),
        P(None, "node"),
        P(None, "node"),
        P("node"),
        P("trade", None),
        P("trade"),
        P("trade"),
        P(),
    )
    out_specs = (P(("trade", "node"), None), P(("trade", "node")), P())
    return jax.shard_map(local, mesh=mesh, in_specs=in_specs, out_specs=out_specs, check_vma=False)
```

profile of v0, /device:TPU:0, one launch (start us, length us, event | category | flops | bytes accessed | tf_op | source)
XLA Modules:
  0.0 175.1 jit_solution(9109322315187114257)
XLA Ops:
  7.2 0.9 bitcast_dynamic-update-slice_fusion.4
  8.1 0.9 bitcast_dynamic-update-slice_fusion.3
  9.0 0.9 bitcast_dynamic-update-slice_fusion.2
  10.0 0.9 bitcast_dynamic-update-slice_fusion.1
  10.9 0.9 bitcast_dynamic-update-slice_fusion
  13.5 5.3 %all-to-all-start = ((f32[8,32,2048]{2,1,0:T(8,128)}), f32[8,32,2048]{2,1,0:T(8,128)S(1)}, u32[]{:S(2)}, u32[]{:S(2)}) async-start(f32[8,32,2048]{2,1,0:T(8,128)} %bitcast.102), calls=%async_computation | async-start | bytes 4194304 | tf_op jit(solution)/shard_map/all_to_all | solution.py:40
  19.2 34.6 %all-to-all-done = f32[8,32,2048]{2,1,0:T(8,128)S(1)} async-done(((f32[8,32,2048]{2,1,0:T(8,128)}), f32[8,32,2048]{2,1,0:T(8,128)S(1)}, u32[]{:S(2)}, u32[]{:S(2)}) %all-to-all-start) | async-done | bytes 2097184 | tf_op jit(solution)/shard_map/all_to_all | solution.py:40
  53.8 1.3 copy-done
  55.1 2.2 %copy.17 = f32[4,8,8,2048]{3,1,2,0:T(8,128)S(1)} copy(f32[4,8,8,2048]{3,1,0,2:T(8,128)} %bitcast.101) | data formatting | bytes 4194304
  57.3 19.5 %all-gather.2.cloned.1.call-done = f32[6,16,16384]{2,1,0:T(8,128)} async-done(((f32[6,16,2048]{2,1,0:T(8,128)}), f32[6,16,16384]{2,1,0:T(8,128)}) %all-gather.2.cloned.1.call-update) | async-done | bytes 6291472 | tf_op jit(solution)/shard_map/all_gather | solution.py:82
  76.8 5.8 %fusion.2 = (f32[1,1,16384]{2,1,0:T(1,128)S(1)}, f32[1,1,16384]{2,1,0:T(1,128)S(1)}, f32[1,1,16384]{2,1,0:T(1,128)S(1)}, f32[1,1,16384]{2,1,0:T(1,128)S(1)}, f32...) fusion(f32[6,16,16384]{2,1,0:T(8,128)} %all-gather.2.cloned.1.c, ...), kind=kLoop, calls=%fused_computation.62 | loop fusion | bytes 2490368 | tf_op jit(solution)/shard_map/slice | solution.py:54
  82.7 5.7 %fusion.3 = (f32[1,1,16384]{2,1,0:T(1,128)S(1)}, f32[1,1,16384]{2,1,0:T(1,128)S(1)}, f32[1,1,16384]{2,1,0:T(1,128)S(1)}, f32[1,1,16384]{2,1,0:T(1,128)S(1)}, f32...) fusion(f32[6,16,16384]{2,1,0:T(8,128)} %all-gather.2.cloned.1.c, ...), kind=kLoop, calls=%fused_computation.63 | loop fusion | bytes 2490368 | tf_op jit(solution)/shard_map/slice | solution.py:54
  88.4 5.5 %fusion.1 = (f32[1,1,16384]{2,1,0:T(1,128)S(1)}, f32[1,1,16384]{2,1,0:T(1,128)S(1)}, f32[1,1,16384]{2,1,0:T(1,128)S(1)}, f32[1,1,16384]{2,1,0:T(1,128)S(1)}, f32...) fusion(f32[6,16,16384]{2,1,0:T(8,128)} %all-gather.2.cloned.1.c, ...), kind=kLoop, calls=%fused_computation.61 | loop fusion | bytes 2490368 | tf_op jit(solution)/shard_map/slice | solution.py:54
  94.1 6.1 %fusion = (f32[1,1,16384]{2,1,0:T(1,128)S(1)}, f32[1,1,16384]{2,1,0:T(1,128)S(1)}, f32[1,1,16384]{2,1,0:T(1,128)S(1)}, f32[1,1,16384]{2,1,0:T(1,128)S(1)}, f32[1...) fusion(f32[6,16,16384]{2,1,0:T(8,128)} %all-gather.2.cloned.1.c, ...), kind=kLoop, calls=%fused_computation.60 | loop fusion | bytes 2490368 | tf_op jit(solution)/shard_map/slice | solution.py:54
  100.2 2.1 %fusion.4 = (f32[1,1,16384]{2,1,0:T(1,128)S(1)}, f32[1,1,16384]{2,1,0:T(1,128)S(1)}, f32[1,1,16384]{2,1,0:T(1,128)S(1)}, f32[1,1,16384]{2,1,0:T(1,128)S(1)}, f32[1,1,16384]{2,1,0:T(1,128)S(1)}) fusion(f32[6,16,16384]{2,1,0:T(8,128)} %all-gather.2.cloned.1.call-done), kind=kLoop, calls=%fused_computation.64 | loop fusion | bytes 655360 | tf_op jit(solution)/shard_map/slice | solution.py:54
  102.4 1.4 maximum_select_fusion.15
  103.8 1.4 maximum_select_fusion.14
  105.2 1.4 maximum_select_fusion.13
  106.6 1.4 maximum_select_fusion.12
  107.9 1.6 maximum_select_fusion.11
  109.5 1.4 maximum_select_fusion.10
  110.9 1.4 maximum_select_fusion.9
  112.3 1.4 maximum_select_fusion.8
  113.7 1.4 maximum_select_fusion.7
  115.1 1.4 maximum_select_fusion.6
  116.5 1.4 maximum_select_fusion.5
  117.9 1.4 maximum_select_fusion.4
  119.3 1.4 maximum_select_fusion.3
  120.6 1.6 maximum_select_fusion.2
  122.2 1.4 maximum_select_fusion.1
  123.6 3.4 %multiply_reduce_fusion = (f32[]{:T(128)}, f32[32]{0:T(128)}, f32[32,16384]{1,0:T(8,128)}) fusion(f32[16384]{0:T(1024)S(1)} %bitcast.169, f32[32]{0:T(128)S(1)} %dynamic_slice.11, f32[16384]{0:T(1024)S(1)} %bitcast.170, f32[16384]{0:T(1024)S(1)} %bitcast.171, f32[32]{0:T(128)S(1)} %dynamic_slice.10, f32[16384]{0:T(1024)S(1)} %bitcast.108, ...), kind=kLoop, calls=%fused_computation.16 | loop fusion | flops 7339999 | bytes 4653476 | tf_op jit(solution)/shard_map/reduce_sum | solution.py:84
  127.0 39.5 %psum.7 = f32[]{:T(128)} all-reduce(f32[]{:T(128)} %get-tuple-element.3), channel_id=1, replica_groups=mesh['trade'=4,'node'=8] {'trade','node'}, use_global_device_ids=true, to_apply=%region_19.20 | all-reduce | flops 1 | bytes 8 | tf_op jit(solution)/shard_map/psum | solution.py:84
  (35 shorter events, 2.2 us)
Async XLA Ops:
  7.2 69.7 %all-gather.2.cloned.1.call-start = ((), (), s32[]{:S(2)}) async-start(), calls=%async_computation.1 | async-start | bytes 7077888 | tf_op jit(solution)/shard_map/all_gather | solution.py:82
  12.5 0.9 copy-start.1
  13.4 5.4 %copy-start.2 = (s32[256]{0:T(256)S(1)}, s32[256]{0:T(256)}, u32[]{:S(2)}) copy-start(s32[256]{0:T(256)} %param.20) | copy-start | bytes 3076
  13.4 5.5 %copy-start.3 = (s32[256]{0:T(256)S(1)}, s32[256]{0:T(256)}, u32[]{:S(2)}) copy-start(s32[256]{0:T(256)} %param.19) | copy-start | bytes 3076
  13.5 5.5 %copy-start.5 = (f32[64]{0:T(128)S(1)}, f32[64]{0:T(128)}, u32[]{:S(2)}) copy-start(f32[64]{0:T(128)} %param.21) | copy-start | bytes 772
  13.5 5.6 %copy-start.4 = (s32[256,4]{0,1:T(4,128)S(1)}, s32[256,4]{0,1:T(4,128)}, u32[]{:S(2)}) copy-start(s32[256,4]{0,1:T(4,128)} %param.18) | copy-start | bytes 12292
  13.5 40.3 %all-to-all-start = ((f32[8,32,2048]{2,1,0:T(8,128)}), f32[8,32,2048]{2,1,0:T(8,128)S(1)}, u32[]{:S(2)}, u32[]{:S(2)}) async-start(f32[8,32,2048]{2,1,0:T(8,128)} %bitcast.102), calls=%async_computation | async-start | bytes 4194304 | tf_op jit(solution)/shard_map/all_to_all | solution.py:40
  53.8 1.3 copy-start
Sparse Core Ops, SparseCore 0:
  13.6 63.2 all-gather.1
where the time goes:
time: 176 us; the launch traced here: 175 us
  waiting for transfers between devices  54.1 us (31%)
  blocking collectives  39.5 us (22%)
  local copies, waits for them, and re-layouts  35.1 us (20%)
  other arithmetic  24.9 us (14%)
  between operations  16.2 us (9%)
  starting transfers between devices  5.38 us (3%)
    psum x1, blocking collectives, local(): lax.psum(jnp.sum(prices), ('trade', 'node')) / values_in.shape[0]  39.5 us
    all_to_all x1, waiting for transfers between devices, to_trade_rows(): lax.all_to_all(blocks, 'node', split_axis=0, concat_axis=2, tiled=True)  34.6 us
    select_n x15, other arithmetic, exercise(): return jnp.where(active[:, None], jnp.maximum(values, payoff), values)  21.1 us
    all_gather x1, waiting for transfers between devices, local(): lattice = lax.all_gather(local_lattice, 'node', axis=2, tiled=True)  19.5 us
    slice x3, local copies, waits for them, and re-layouts, roll_back(): lattice[2, local_step]  14 us
    slice x2, local copies, waits for them, and re-layouts, roll_back(): lattice[0, local_step]  11.2 us
    unnamed x18, local copies, waits for them, and re-layouts  9.01 us
    all_to_all x1, starting transfers between devices, to_trade_rows(): lax.all_to_all(blocks, 'node', split_axis=0, concat_axis=2, tiled=True)  5.34 us
  transfers between devices with their start and end apart: 2, of which 2 were waited for; matrix products, arithmetic and copies ran while one was open for 1% of the time, Pallas kernels for 0%

commit v1 on v0

--- a/solution.py
+++ b/solution.py
@@ -79,7 +79,7 @@
     signs = (2 * notional_sign - 1).astype(jnp.float32)
     values = to_trade_rows(values_in)
     local_lattice = stack_lattice(prob_up, prob_down, discount, swap_rate, annuity, state_price, 0)
-    lattice = lax.all_gather(local_lattice, "node", axis=2, tiled=True)
+    lattice = jnp.concatenate(lax.all_gather(local_lattice, "node"), 2)
     values, prices = roll_back(values, lattice, exercise_step, strike, signs, 0, step_count)
     portfolio = lax.psum(jnp.sum(prices), ("trade", "node")) / values_in.shape[0]
     return (values, prices, portfolio)

time: 176 us -> 192 us (1.091)
  local copies, waits for them, and re-layouts: 35.1 us -> 51.4 us
    all_gather x0 -> x1, local copies, waits for them, and re-layouts: none -> 9.14 us  [local(): lattice = jnp.concatenate(lax.all_gather(local_lattice, 'node'), 2)]
    reshape x0 -> x1, local copies, waits for them, and re-layouts: none -> 7.18 us  [local(): lattice = jnp.concatenate(lax.all_gather(local_lattice, 'node'), 2)]
where the time goes in v1:
time: 192 us
  waiting for transfers between devices  54.1 us (28%)
  local copies, waits for them, and re-layouts  51.4 us (27%)
  blocking collectives  39.5 us (21%)
  other arithmetic  25 us (13%)
  between operations  16.2 us (8%)
  starting transfers between devices  5.38 us (3%)
    psum x1, blocking collectives, local(): lax.psum(jnp.sum(prices), ('trade', 'node')) / values_in.shape[0]  39.5 us
    all_to_all x1, waiting for transfers between devices, to_trade_rows(): lax.all_to_all(blocks, 'node', split_axis=0, concat_axis=2, tiled=True)  34.6 us
    select_n x15, other arithmetic, exercise(): return jnp.where(active[:, None], jnp.maximum(values, payoff), values)  21.2 us
    all_gather x1, waiting for transfers between devices, local(): lattice = jnp.concatenate(lax.all_gather(local_lattice, 'node'), 2)  19.5 us
    slice x3, local copies, waits for them, and re-layouts, roll_back(): lattice[2, local_step]  14 us
    slice x2, local copies, waits for them, and re-layouts, roll_back(): lattice[0, local_step]  11.2 us
    all_gather x1, local copies, waits for them, and re-layouts, local(): lattice = jnp.concatenate(lax.all_gather(local_lattice, 'node'), 2)  9.14 us
    unnamed x18, local copies, waits for them, and re-layouts  9.01 us
  transfers between devices with their start and end apart: 2, of which 2 were waited for; matrix products, arithmetic and copies ran while one was open for 1% of the time, Pallas kernels for 0%

profile of v1, /device:TPU:0, one launch (start us, length us, event | category | flops | bytes accessed | tf_op | source)
XLA Modules:
  0.0 191.5 jit_solution(5548511773800435310)
XLA Ops:
  8.1 0.9 bitcast_dynamic-update-slice_fusion.3
  9.0 0.9 bitcast_dynamic-update-slice_fusion.2
  10.9 0.9 bitcast_dynamic-update-slice_fusion
  13.5 5.3 %all-to-all-start = ((f32[8,32,2048]{2,1,0:T(8,128)}), f32[8,32,2048]{2,1,0:T(8,128)S(1)}, u32[]{:S(2)}, u32[]{:S(2)}) async-start(f32[8,32,2048]{2,1,0:T(8,128)} %bitcast.110), calls=%async_computation | async-start | bytes 4194304 | tf_op jit(solution)/shard_map/all_to_all | solution.py:40
  19.2 34.6 %all-to-all-done = f32[8,32,2048]{2,1,0:T(8,128)S(1)} async-done(((f32[8,32,2048]{2,1,0:T(8,128)}), f32[8,32,2048]{2,1,0:T(8,128)S(1)}, u32[]{:S(2)}, u32[]{:S(2)}) %all-to-all-start) | async-done | bytes 2097184 | tf_op jit(solution)/shard_map/all_to_all | solution.py:40
  53.8 1.3 copy-done
  55.1 2.2 %copy.22 = f32[4,8,8,2048]{3,1,2,0:T(8,128)S(1)} copy(f32[4,8,8,2048]{3,1,0,2:T(8,128)} %bitcast.108) | data formatting | bytes 4194304
  57.3 19.5 %all-gather.3.cloned.1.call-done = f32[48,16,2048]{2,1,0:T(8,128)} async-done(((f32[6,16,2048]{2,1,0:T(8,128)}), f32[48,16,2048]{2,1,0:T(8,128)}) %all-gather.3.cloned.1.call-update) | async-done | bytes 6291472 | tf_op jit(solution)/shard_map/all_gather | solution.py:82
  76.8 9.1 %copy.25 = f32[8,6,16,2048]{3,0,2,1:T(8,128)} copy(f32[8,6,16,2048]{3,2,1,0:T(8,128)} %bitcast.109) | data formatting | bytes 12582912 | tf_op jit(solution)/shard_map/all_gather | solution.py:82
  86.0 7.2 %reshape.281 = f32[6,16,16384]{2,1,0:T(8,128)} reshape(f32[6,16,8,2048]{3,2,1,0:T(8,128)} %bitcast.106) | data formatting | bytes 12582912 | tf_op jit(solution)/shard_map/reshape | solution.py:82
  93.1 5.8 %fusion.2 = (f32[1,1,16384]{2,1,0:T(1,128)S(1)}, f32[1,1,16384]{2,1,0:T(1,128)S(1)}, f32[1,1,16384]{2,1,0:T(1,128)S(1)}, f32[1,1,16384]{2,1,0:T(1,128)S(1)}, f32...) fusion(f32[6,16,16384]{2,1,0:T(8,128)} %reshape.281), kind=kLoop, calls=%fused_computation.63 | loop fusion | bytes 2490368 | tf_op jit(solution)/shard_map/slice | solution.py:54
  98.9 5.7 %fusion.3 = (f32[1,1,16384]{2,1,0:T(1,128)S(1)}, f32[1,1,16384]{2,1,0:T(1,128)S(1)}, f32[1,1,16384]{2,1,0:T(1,128)S(1)}, f32[1,1,16384]{2,1,0:T(1,128)S(1)}, f32...) fusion(f32[6,16,16384]{2,1,0:T(8,128)} %reshape.281), kind=kLoop, calls=%fused_computation.64 | loop fusion | bytes 2490368 | tf_op jit(solution)/shard_map/slice | solution.py:54
  104.6 5.5 %fusion.1 = (f32[1,1,16384]{2,1,0:T(1,128)S(1)}, f32[1,1,16384]{2,1,0:T(1,128)S(1)}, f32[1,1,16384]{2,1,0:T(1,128)S(1)}, f32[1,1,16384]{2,1,0:T(1,128)S(1)}, f32...) fusion(f32[6,16,16384]{2,1,0:T(8,128)} %reshape.281), kind=kLoop, calls=%fused_computation.62 | loop fusion | bytes 2490368 | tf_op jit(solution)/shard_map/slice | solution.py:54
  110.2 6.1 %fusion = (f32[1,1,16384]{2,1,0:T(1,128)S(1)}, f32[1,1,16384]{2,1,0:T(1,128)S(1)}, f32[1,1,16384]{2,1,0:T(1,128)S(1)}, f32[1,1,16384]{2,1,0:T(1,128)S(1)}, f32[1...) fusion(f32[6,16,16384]{2,1,0:T(8,128)} %reshape.281), kind=kLoop, calls=%fused_computation.61 | loop fusion | bytes 2490368 | tf_op jit(solution)/shard_map/slice | solution.py:54
  116.3 2.1 %fusion.4 = (f32[1,1,16384]{2,1,0:T(1,128)S(1)}, f32[1,1,16384]{2,1,0:T(1,128)S(1)}, f32[1,1,16384]{2,1,0:T(1,128)S(1)}, f32[1,1,16384]{2,1,0:T(1,128)S(1)}, f32[1,1,16384]{2,1,0:T(1,128)S(1)}) fusion(f32[6,16,16384]{2,1,0:T(8,128)} %reshape.281), kind=kLoop, calls=%fused_computation.65 | loop fusion | bytes 655360 | tf_op jit(solution)/shard_map/slice | solution.py:54
  118.7 1.4 maximum_select_fusion.15
  120.1 1.4 maximum_select_fusion.14
  121.5 1.4 maximum_select_fusion.13
  122.9 1.4 maximum_select_fusion.12
  124.3 1.4 maximum_select_fusion.11
  125.7 1.6 maximum_select_fusion.10
  127.3 1.4 maximum_select_fusion.9
  128.6 1.4 maximum_select_fusion.8
  130.0 1.4 maximum_select_fusion.7
  131.4 1.4 maximum_select_fusion.6
  132.8 1.4 maximum_select_fusion.5
  134.2 1.4 maximum_select_fusion.4
  135.6 1.4 maximum_select_fusion.3
  137.0 1.4 maximum_select_fusion.2
  138.4 1.6 maximum_select_fusion.1
  140.0 3.4 %multiply_reduce_fusion = (f32[]{:T(128)}, f32[32]{0:T(128)}, f32[32,16384]{1,0:T(8,128)}) fusion(f32[16384]{0:T(1024)S(1)} %bitcast.177, f32[32]{0:T(128)S(1)} %dynamic_slice.11, f32[16384]{0:T(1024)S(1)} %bitcast.178, f32[16384]{0:T(1024)S(1)} %bitcast.179, f32[32]{0:T(128)S(1)} %dynamic_slice.10, f32[16384]{0:T(1024)S(1)} %bitcast.116, ...), kind=kLoop, calls=%fused_computation.17 | loop fusion | flops 7339999 | bytes 4653476 | tf_op jit(solution)/shard_map/reduce_sum | solution.py:84
  143.4 39.5 %psum.7 = f32[]{:T(128)} all-reduce(f32[]{:T(128)} %get-tuple-element.3), channel_id=1, replica_groups=mesh['trade'=4,'node'=8] {'trade','node'}, use_global_device_ids=true, to_apply=%region_19.20 | all-reduce | flops 1 | bytes 8 | tf_op jit(solution)/shard_map/psum | solution.py:84
  (37 shorter events, 4.0 us)
Async XLA Ops:
  7.2 69.7 %all-gather.3.cloned.1.call-start = ((), (), s32[]{:S(2)}) async-start(), calls=%async_computation.1 | async-start | bytes 7077888 | tf_op jit(solution)/shard_map/all_gather | solution.py:82
  12.5 0.9 copy-start.1
  13.4 5.4 %copy-start.2 = (s32[256]{0:T(256)S(1)}, s32[256]{0:T(256)}, u32[]{:S(2)}) copy-start(s32[256]{0:T(256)} %param.20) | copy-start | bytes 3076
  13.4 5.5 %copy-start.3 = (s32[256]{0:T(256)S(1)}, s32[256]{0:T(256)}, u32[]{:S(2)}) copy-start(s32[256]{0:T(256)} %param.19) | copy-start | bytes 3076
  13.5 5.5 %copy-start.5 = (f32[64]{0:T(128)S(1)}, f32[64]{0:T(128)}, u32[]{:S(2)}) copy-start(f32[64]{0:T(128)} %param.21) | copy-start | bytes 772
  13.5 5.6 %copy-start.4 = (s32[256,4]{0,1:T(4,128)S(1)}, s32[256,4]{0,1:T(4,128)}, u32[]{:S(2)}) copy-start(s32[256,4]{0,1:T(4,128)} %param.18) | copy-start | bytes 12292
  13.5 40.3 %all-to-all-start = ((f32[8,32,2048]{2,1,0:T(8,128)}), f32[8,32,2048]{2,1,0:T(8,128)S(1)}, u32[]{:S(2)}, u32[]{:S(2)}) async-start(f32[8,32,2048]{2,1,0:T(8,128)} %bitcast.110), calls=%async_computation | async-start | bytes 4194304 | tf_op jit(solution)/shard_map/all_to_all | solution.py:40
  53.8 1.3 copy-start
Sparse Core Ops, SparseCore 0:
  13.6 63.2 all-gather.2
